TPU v7x, 128 devices: a whole 4x4x4 slice. The times are simulated.
128 devices in a mesh: leaf: 128 (over z, x, y, core).
Axes of the slice: x: 4, y: 4, z: 4, core: 2. Of those that a mesh axis runs over, the one named last changes fastest.
Arguments:
- coords: float32 [3, 1048576], P(None, 'leaf'), may hold values from 0 to 1
- charges: bfloat16 [1048576, 128], P('leaf'), may hold values from -6 to 6
- near_leaves: int32 [8192, 27], P('leaf'), may hold values from 0 to 191
- leaf_basis: bfloat16 [8192, 4096], P('leaf'), may hold values from -1 to 1
- leaf_transfer: bfloat16 [8192, 1024], P('leaf'), may hold values from -0.75 to 0.75
- mid_transfer: bfloat16 [1024, 1024], P('leaf'), may hold values from -0.75 to 0.75
- base_transfer: bfloat16 [128, 1024], P('leaf'), may hold values from -0.75 to 0.75
- base_coupling: bfloat16 [24192, 1024], P('leaf'), may hold values from -0.01953125 to 0.01953125
- base_target: int32 [24192, 1], P('leaf'), may hold values from 0 to 127; in each aligned block of 189 rows (0 to 188, 189 to 377, ...) at most 2 rows name the same one
- base_source: int32 [24192], P('leaf'), may hold values from 0 to 127
- top_coupling: bfloat16 [1024, 1024], P('leaf'), may hold values from -0.015625 to 0.015625
- top_target: int32 [1024], P('leaf'), may hold values from 0 to 15
- top_source: int32 [1024], P('leaf'), may hold values from 0 to 15
Outputs:
- potential: bfloat16 [1048576, 128], P('leaf')
Inputs may be any that keep to these rules, and one draw needn't show every extreme that they name: `near_leaves`: entry j of leaf l names leaf 64 * (l // 64 - 1) + j: a leaf of the device before in Morton order, of the row's own device, or of the device after; repeats may occur. `base_target`: among the 189 blocks of one device no base cluster is the target more than 2 times; that count is reached.
All inputs are finite; a program needn't handle non-finite values.
Results may differ from a plain program's by a relative error of at most 0.01.
Values may be sent and summed in bfloat16 or wider, within the bound.
A program may use at most 128 MiB of HBM per device.

v0:
```python
import functools
import math

import jax
import jax.numpy as jnp
from jax import lax
from jax.experimental import pallas as pl
from jax.experimental.pallas import tpu as pltpu
from jax.sharding import PartitionSpec as P

K = 32
RHS = 128
M = 128
N = 128
LEAVES = 64
POOL = 3 * LEAVES
NNEAR = 27
HALF = (NNEAR + 1) // 2
GROUP = 8
DELTA_SQ = 0.0025
AXIS = "leaf"
MESH = pl.DeviceIdType.MESH
bf16 = jnp.bfloat16
f32 = jnp.float32


def dot(a, b):
    return jnp.dot(a, b, preferred_element_type=f32)


def dot_t(a, b):
    return lax.dot_general(a, b, (((0,), (0,)), ((), ())), preferred_element_type=f32)


def vmem(*shape):
    return pl.BlockSpec(shape, lambda *_: (0,) * len(shape))


def split3(v):
    high = v.astype(bf16).astype(f32)
    rest = v - high
    mid = rest.astype(bf16).astype(f32)
    return high, mid, rest - mid


def features(scale, points, target):
    centred = [(p - 0.5) * scale for p in points]
    norm = centred[0] * centred[0] + centred[1] * centred[1] + centred[2] * centred[2]
    one = jnp.ones_like(norm)
    rows = []
    for c in centred:
        h, m, l = split3(c)
        if target:
            h, m, l = -2.0 * h, -2.0 * m, -2.0 * l
            rows += [h, h, m, m, h, l]
        else:
            rows += [h, m, h, m, l, h]
    if target:
        rows += [*split3(norm + scale * scale * DELTA_SQ), one, one, one]
    else:
        rows += [one, one, one, *split3(norm)]
    return rows + [jnp.zeros_like(norm)] * (K - len(rows))


def exchange_kernel(
    scale,
    near,
    blk,
    blk_src,
    top,
    top_idx,
    coords,
    charges,
    basis,
    transfers,
    r_blk,
    r_src,
    every,
    top_all,
    top_sum,
    source,
    target,
    partner,
    other,
    partial,
    pool,
    kern,
    gathered,
    sums,
    points,
    half,
    half_src,
    tops,
    r_top,
    r_idx,
    lifted,
    coeffs,
    mine,
    mids,
    part,
    others,
    lines,
    send,
    recv,
    local,
    leave,
):
    me = lax.axis_index(AXIS)
    plane, place = me // GROUP, me % GROUP
    core, y = place % 2, place // 2
    held = pool.at[pl.ds(0, LEAVES)]
    fetch = pltpu.make_async_copy(charges, held, local.at[0])
    fetch.start()
    barrier = pltpu.get_barrier_semaphore()

    across_chip, next_chip = me + 1 - 2 * core, lax.rem(me - 1 + 2 * core + N, N)
    peers = [plane * GROUP + lax.rem(place + o, GROUP) for o in range(1, GROUP)]
    planes = [lax.rem(plane + o, 16) for o in range(1, 16)]
    greeted = [*peers, *[p * GROUP + place for p in planes], next_chip]
    for to in greeted:
        pl.semaphore_signal(barrier, inc=1, device_id=(to,), device_id_type=MESH)
    for i in range(3):
        for l in range(LEAVES):
            points[i, l : l + 1, :] = coords[i : i + 1, l * M : (l + 1) * M]
    pool[2 * LEAVES] = jnp.zeros((M, RHS), bf16)

    fetch.wait()

    def one_mid(m, c):
        rows = []
        for b in range(GROUP):
            rows.append(dot(basis[m * GROUP + b], pool[m * GROUP + b]).astype(bf16))
        first = pl.multiple_of(m * GROUP * K, GROUP * K)
        rows = dot_t(transfers[pl.ds(first, GROUP * K), :], jnp.concatenate(rows, axis=0))
        mids[pl.ds(pl.multiple_of(m * K, K), K), :] = rows.astype(bf16)
        return c

    lax.fori_loop(0, GROUP, one_mid, 0)
    base = dot_t(transfers[LEAVES * K : LEAVES * K + GROUP * K, :], mids[...]).astype(bf16)
    coeffs[0] = base
    coeffs[1] = dot_t(transfers[LEAVES * K + GROUP * K :, :], base).astype(bf16)
    pl.semaphore_wait(barrier, len(greeted))

    def remote(src, dst, k, to):
        return pltpu.make_async_remote_copy(
            src_ref=src,
            dst_ref=dst,
            send_sem=send.at[k],
            recv_sem=recv.at[k],
            device_id=(to,),
            device_id_type=MESH,
        )

    def finish(ref, k):
        whole = remote(ref, ref, k, me)
        whole.wait_send()
        whole.wait_recv()

    for o in range(1, 4):
        to = plane * GROUP + lax.rem(y + o, 4) * 2 + core
        remote(coeffs.at[0], every.at[core, plane, y], 6, to).start()
    for to in peers:
        remote(coeffs.at[1], lifted.at[place], 7, to).start()
    for to in peers:
        remote(blk.at[to % GROUP], half.at[place], 4, to).start()
        remote(blk_src.at[to % GROUP], half_src.at[place], 5, to).start()
    to_partner = remote(points, others.at[0], 0, across_chip)
    to_other = remote(points, others.at[1], 1, next_chip)
    to_partner.start()
    to_other.start()
    swap = remote(held, pool.at[pl.ds(LEAVES, LEAVES)], 12, across_chip)
    swap.start()
    for p in planes:
        to = p * GROUP + place
        remote(top, r_top.at[plane], 2, to).start()
        remote(top_idx, r_idx.at[plane], 3, to).start()
    outward = remote(held, other, 13, next_chip)
    outward.start()
    own = [
        pltpu.make_async_copy(blk.at[place], half.at[place], local.at[1]),
        pltpu.make_async_copy(blk_src.at[place], half_src.at[place], local.at[2]),
        pltpu.make_async_copy(top, r_top.at[plane], local.at[3]),
        pltpu.make_async_copy(top_idx, r_idx.at[plane], local.at[4]),
        pltpu.make_async_copy(coeffs.at[0], every.at[core, plane, y], local.at[5]),
        pltpu.make_async_copy(coeffs.at[1], lifted.at[place], local.at[6]),
    ]
    for copy in own:
        copy.start()

    def side(rows, put, count):
        for r, row in enumerate(rows):
            lines[pl.ds(r, LEAVES, stride=K), :] = row
        lax.fori_loop(0, count, put, 0, unroll=4)

    def line(l):
        return lines[pl.ds(pl.multiple_of(l * K, K), K), :]

    def put_target(l, c):
        target[l] = line(l).T.astype(bf16)
        return c

    def put_source(block):
        def put(l, c):
            source[block * LEAVES + l] = line(l).astype(bf16)
            return c

        return put

    here = [points[i] for i in range(3)]
    side(features(scale, here, True), put_target, LEAVES)
    for copy in own:
        copy.wait()
    finish(lifted.at[pl.ds(0, 3)], 6)
    for p in planes:
        to = p * GROUP + place
        remote(every.at[core, plane], every.at[core, plane], 8, to).start()
    finish(lifted.at[pl.ds(0, GROUP - 1)], 7)
    mine[...] = jnp.sum(lifted[...].astype(f32), axis=0).astype(bf16)
    for p in planes:
        remote(mine, top_all.at[plane], 9, p * GROUP + place).start()
    own_top = pltpu.make_async_copy(mine, top_all.at[plane], local.at[0])
    own_top.start()
    side(features(scale, here, False), put_source(0), LEAVES)
    own_top.wait()

    finish(half.at[pl.ds(0, GROUP - 1)], 4)
    finish(half_src.at[pl.ds(0, GROUP - 1)], 5)
    for p in planes:
        to = p * GROUP + place
        remote(half.at[:, p], r_blk.at[plane], 14, to).start()
        remote(half_src.at[:, p], r_src.at[plane], 15, to).start()
    own = [
        pltpu.make_async_copy(half.at[:, plane], r_blk.at[plane], local.at[2]),
        pltpu.make_async_copy(half_src.at[:, plane], r_src.at[plane], local.at[3]),
    ]
    for copy in own:
        copy.start()
    to_partner.wait()
    to_other.wait()
    spare = source[0]
    for l in range(8):
        source[POOL + l] = spare
    for i in range(2):
        side(features(scale, [others[i, j] for j in range(3)], False), put_source(i + 1), LEAVES)

    swap.wait()
    keep = pltpu.make_async_copy(pool.at[pl.ds(LEAVES, LEAVES)], partner, local.at[1])
    keep.start()

    def close_group(group, c):
        for b in range(GROUP):
            leaf = group * GROUP + b
            for j in range(HALF // 2):
                one, two = near[leaf, 2 * j], near[leaf, 2 * j + 1]
                pair_rows(
                    b, target[leaf], one, two, j, source, pool, kern, gathered, 2 * LEAVES
                )
            sums[leaf] = dot(kern[b], gathered[b])
        return c

    lax.fori_loop(0, 2, close_group, 0)

    finish(r_top.at[pl.ds(0, 15)], 2)
    finish(r_idx.at[pl.ds(0, 15)], 3)
    named = jnp.sum(r_idx[...], axis=0)
    wanted = plane * 16 + lax.broadcasted_iota(jnp.int32, (16, N), 0)
    chosen = jnp.where(wanted == named, 1.0, 0.0).astype(bf16)
    part[...] = dot(chosen, r_top[...].reshape(N, K * K)).astype(bf16)
    for to in peers:
        remote(part, tops.at[place], 10, to).start()
    own_part = pltpu.make_async_copy(part, tops.at[place], local.at[0])
    own_part.start()

    lax.fori_loop(2, 4, close_group, 0)
    finish(every.at[0, pl.ds(0, 15)], 8)
    across = remote(every.at[core], every.at[core], 11, across_chip)
    across.start()
    lax.fori_loop(4, 6, close_group, 0)
    own_part.wait()
    finish(tops.at[pl.ds(0, GROUP - 1)], 10)
    top_sum[...] = jnp.sum(tops[...].astype(f32), axis=0)
    lax.fori_loop(6, GROUP, close_group, 0)
    away = pltpu.make_async_copy(sums, partial, leave)
    away.start()
    finish(top_all.at[pl.ds(0, 15)], 9)
    across.wait()
    for copy in own:
        copy.wait()
    finish(r_blk.at[pl.ds(0, 15)], 14)
    finish(r_src.at[pl.ds(0, 15)], 15)
    keep.wait()
    away.wait()
    outward.wait()


def exchange_call(near, blk, blk_src, top, top_idx, coords, charges, basis, transfers):
    inside = pl.BlockSpec(memory_space=pltpu.VMEM)
    anywhere = pl.BlockSpec(memory_space=pl.ANY)
    shape = jax.ShapeDtypeStruct
    return pl.pallas_call(
        functools.partial(exchange_kernel, math.sqrt(NNEAR * M)),
        out_shape=(
            shape((16, GROUP, *blk.shape[2:]), bf16),
            shape((16, GROUP, *blk_src.shape[2:]), jnp.int32),
            shape((2, 16, 4, K, RHS), bf16),
            shape((16, K, RHS), bf16),
            shape((16, K * K), f32),
            shape((POOL + 8, K, M), bf16),
            shape((LEAVES, M, K), bf16),
            shape((LEAVES, M, RHS), bf16),
            shape((LEAVES, M, RHS), bf16),
            shape((LEAVES, M, RHS), f32),
        ),
        in_specs=[
            pl.BlockSpec(memory_space=pltpu.SMEM),
            *[inside] * 5,
            anywhere,
            inside,
            inside,
        ],
        out_specs=(*[inside] * 7, *[anywhere] * 3),
        scratch_shapes=[
            pltpu.VMEM((2 * LEAVES + 1, M, RHS), bf16),
            pltpu.VMEM((GROUP, M, M * HALF), bf16),
            pltpu.VMEM((GROUP, M * HALF, RHS), bf16),
            pltpu.VMEM((LEAVES, M, RHS), f32),
            pltpu.VMEM((3, LEAVES, M), f32),
            pltpu.VMEM(blk.shape, bf16),
            pltpu.VMEM(blk_src.shape, jnp.int32),
            pltpu.VMEM((GROUP, 16, K * K), bf16),
            pltpu.VMEM((16, 8, K * K), bf16),
            pltpu.VMEM((16, 1, N), jnp.int32),
            pltpu.VMEM((GROUP, K, RHS), bf16),
            pltpu.VMEM((2, K, RHS), bf16),
            pltpu.VMEM((K, RHS), bf16),
            pltpu.VMEM((GROUP * K, RHS), bf16),
            pltpu.VMEM((16, K * K), bf16),
            pltpu.VMEM((2, 3, LEAVES, M), f32),
            pltpu.VMEM((LEAVES * K, M), f32),
            pltpu.SemaphoreType.DMA((16,)),
            pltpu.SemaphoreType.DMA((16,)),
            pltpu.SemaphoreType.DMA((7,)),
            pltpu.SemaphoreType.DMA,
        ],
        compiler_params=pltpu.CompilerParams(
            collective_id=0, has_side_effects=True, vmem_limit_bytes=63 * 1024 * 1024
        ),
        cost_estimate=pl.CostEstimate(flops=10**9, bytes_accessed=10**7, transcendentals=0),
        name="exchange",
    )(near, blk, blk_src, top, top_idx, coords, charges, basis, transfers)


def pair_rows(slot, mine, one, two, j, source, pool, kern, gathered, last):
    squares = dot(mine, jnp.concatenate([source[one], source[two]], axis=1))
    kern[slot, :, 2 * M * j : 2 * M * (j + 1)] = lax.rsqrt(squares.astype(bf16))
    gathered[slot, 2 * M * j : 2 * M * j + M] = pool[jnp.minimum(one, last)]
    gathered[slot, 2 * M * j + M : 2 * M * (j + 1)] = pool[jnp.minimum(two, last)]


def load_pool(refs, pool, sems):
    copies = [
        pltpu.make_async_copy(ref, pool.at[pl.ds(LEAVES * i, LEAVES)], sems.at[i])
        for i, ref in enumerate(refs)
    ]
    for copy in copies:
        copy.start()
    pool[POOL] = jnp.zeros((M, RHS), bf16)
    return copies


def near_kernel(
    near,
    source,
    target,
    here,
    partner,
    other,
    partial,
    a_high,
    a_low,
    every,
    t_high,
    t_low,
    top_all,
    transfers,
    basis,
    out,
    pool,
    kern,
    gathered,
    base,
    extra,
    sems,
):
    step = pl.program_id(0)

    @pl.when(step == 0)
    def _():
        copies = load_pool((here, partner, other), pool, sems)
        extra[...] = jnp.zeros_like(extra)
        top_field = (dot(t_high[...], top_all[...]) + dot(t_low[...], top_all[...])).astype(bf16)
        coupled = dot(a_high[...], every[...]) + dot(a_low[...], every[...])
        base[...] = (coupled + dot(transfers[(LEAVES + GROUP) * K :, :], top_field)).astype(bf16)
        for copy in copies:
            copy.wait()

        @pl.when(near[0, 2 * HALF + 1] > 0)
        def _():
            pool[pl.ds(2 * LEAVES, LEAVES)] = jnp.zeros((LEAVES, M, RHS), bf16)

    late = jnp.int32(0)
    for b in range(GROUP):
        late += HALF - near[step * GROUP + b, 2 * HALF]

    @pl.when(late > 0)
    def _():
        def one_leaf(b, c):
            leaf = step * GROUP + b

            def one_entry(e, total):
                g = near[leaf, e]
                squares = dot(target[b], source[g])
                return total + dot(lax.rsqrt(squares.astype(bf16)), pool[g])

            extra[b] = lax.fori_loop(
                near[leaf, 2 * HALF], HALF, one_entry, jnp.zeros((M, RHS), f32)
            )
            return c

        lax.fori_loop(0, GROUP, one_leaf, 0)

    down = transfers[pl.ds(pl.multiple_of((LEAVES + step) * K, K), K), :]
    mid = dot(down, base[...]).astype(bf16)
    down = transfers[pl.ds(pl.multiple_of(step * GROUP * K, GROUP * K), GROUP * K), :]
    fields = dot(down, mid).astype(bf16)
    for b in range(GROUP):
        leaf = step * GROUP + b
        for j in range(HALF // 2):
            one, two = near[leaf, HALF + 2 * j], near[leaf, HALF + 2 * j + 1]
            pair_rows(b, target[b], one, two, j, source, pool, kern, gathered, POOL)
        far = dot_t(basis[b], fields[b * K : (b + 1) * K])
        total = dot(kern[b], gathered[b]) + far + (partial[b] + extra[b])
        out[pl.ds(b * M, M), :] = total.astype(bf16)

    @pl.when(late > 0)
    def _():
        extra[...] = jnp.zeros_like(extra)


def near_scratch():
    return [
        pltpu.VMEM((POOL + 1, M, RHS), bf16),
        pltpu.VMEM((GROUP, M, M * HALF), bf16),
        pltpu.VMEM((GROUP, M * HALF, RHS), bf16),
    ]


NEAR_PARAMS = dict(
    compiler_params=pltpu.CompilerParams(
        vmem_limit_bytes=63 * 1024 * 1024, dimension_semantics=("arbitrary",)
    ),
    cost_estimate=pl.CostEstimate(
        flops=5 * 10**9, bytes_accessed=10**7, transcendentals=10**7
    ),
)


def near_call(near, source, target, here, partner, other, partial, far, transfers, basis):
    anywhere = pl.BlockSpec(memory_space=pl.ANY)
    grid_spec = pltpu.PrefetchScalarGridSpec(
        num_scalar_prefetch=1,
        grid=(LEAVES // GROUP,),
        in_specs=[
            vmem(*source.shape),
            pl.BlockSpec((GROUP, M, K), lambda i, _: (i, 0, 0)),
            anywhere,
            anywhere,
            anywhere,
            pl.BlockSpec((GROUP, M, RHS), lambda i, _: (i, 0, 0)),
            *[vmem(*v.shape) for v in far],
            vmem(*transfers.shape),
            pl.BlockSpec((GROUP, K, M), lambda i, _: (i, 0, 0)),
        ],
        out_specs=pl.BlockSpec((GROUP * M, RHS), lambda i, _: (i, 0)),
        scratch_shapes=[
            *near_scratch(),
            pltpu.VMEM((K, RHS), bf16),
            pltpu.VMEM((GROUP, M, RHS), f32),
            pltpu.SemaphoreType.DMA((3,)),
        ],
    )
    return pl.pallas_call(
        near_kernel,
        grid_spec=grid_spec,
        out_shape=jax.ShapeDtypeStruct((LEAVES * M, RHS), bf16),
        name="near",
        **NEAR_PARAMS,
    )(near, source, target, here, partner, other, partial, *far, transfers, basis)


def near_lists(near_leaves, core, edge):
    block, inside = near_leaves // LEAVES, near_leaves % LEAVES
    moved = jnp.where(block == 1, 0, jnp.where((block == 0) == (core == 0), 2, 1))
    place = moved * LEAVES + inside
    away = place >= 2 * LEAVES
    column = jnp.arange(NNEAR)
    key = jnp.where(away, NNEAR, 0) + column
    rank = jnp.sum(key[:, None, :] < key[:, :, None], axis=2)
    ordered = jnp.sum(
        jnp.where(rank[:, :, None] == jnp.arange(2 * HALF), place[:, :, None] + 1, 0), axis=1
    )
    ordered = jnp.where(ordered == 0, POOL, ordered - 1)
    ready = jnp.minimum(NNEAR - jnp.sum(away, axis=1, keepdims=True), HALF)
    return jnp.concatenate([ordered, ready, jnp.full_like(ready, edge)], axis=1)


def high_low(v):
    high = v.astype(bf16)
    return high, (v - high.astype(f32)).astype(bf16)


def per_device(
    coords,
    charges,
    near_leaves,
    leaf_basis,
    leaf_transfer,
    mid_transfer,
    base_transfer,
    base_coupling,
    base_target,
    base_source,
    top_coupling,
    top_target,
    top_source,
):
    me = lax.axis_index(AXIS)
    rows = charges.reshape(LEAVES, M, RHS)
    targets = base_target[:, 0]
    count = targets.shape[0]
    earlier = jnp.arange(count)[:, None] > jnp.arange(count)[None, :]
    rank = jnp.sum((targets[:, None] == targets[None, :]) & earlier, axis=1)
    slots = jnp.arange(2 * N)
    places = (targets % GROUP) * 16 + targets // GROUP
    chosen = (slots[:, None] == (2 * places + rank)[None, :]).astype(bf16)
    blk = dot(chosen, base_coupling).astype(bf16).reshape(GROUP, 16, 16, 128)
    order = (base_source % 2) * 64 + (base_source // 8) * 4 + (base_source // 2) % 4
    slot_source = jnp.sum(chosen.astype(jnp.int32) * (order + 1)[None, :], axis=1) - 1
    blk_src = jnp.pad(slot_source.reshape(GROUP, 16, 1, 2), ((0, 0),) * 3 + ((0, 126),))
    lane = jnp.arange(N)
    top_idx = jnp.tile(top_target * 16 + top_source, 16)
    top_idx = jnp.where(lane // 8 == me // GROUP, top_idx, 0).reshape(1, N)

    basis = leaf_basis.reshape(LEAVES, K, M)
    transfers = jnp.concatenate([leaf_transfer, mid_transfer, base_transfer], axis=0)
    transfers = transfers.reshape((LEAVES + GROUP + 1) * K, K)
    edge = ((me == 0) | (me == N - 1)).astype(jnp.int32)
    near = near_lists(near_leaves, me % 2, edge)
    r_blk, r_src, every, top_all, t, source, target, partner, other, partial = exchange_call(
        near, blk, blk_src, top_coupling, top_idx, coords, rows, basis, transfers
    )
    by_source = (lane[:, None] == r_src[:, :, 0, :2].reshape(1, 2 * N)).astype(bf16)
    a = dot(by_source, r_blk.reshape(2 * N, K * K))
    a = a.reshape(N, K, K).transpose(1, 0, 2).reshape(K, N * K)
    t = t.reshape(16, K, K).transpose(1, 0, 2).reshape(K, 16 * K)
    far = (
        *high_low(a),
        every.reshape(N * K, RHS),
        *high_low(t),
        top_all.reshape(16 * K, RHS),
    )
    return near_call(
        near, source, target, rows, partner, other, partial, far, transfers, basis
    )


def solution(mesh):
    lead = P(AXIS, None)
    in_specs = (
        P(None, AXIS),
        lead,
        lead,
        lead,
        lead,
        lead,
        lead,
        lead,
        lead,
        P(AXIS),
        lead,
        P(AXIS),
        P(AXIS),
    )
    return jax.shard_map(
        per_device, mesh=mesh, in_specs=in_specs, out_specs=lead, check_vma=False
    )
```

profile of v0, /device:TPU:102, one launch (start us, length us, event | category | flops | bytes accessed | tf_op | source)
XLA Modules:
  0.0 109.3 jit_solution(12877728601951742904)
XLA Ops:
  0.0 0.0 copy-start
  0.0 0.0 copy-start.1
  0.0 0.1 pad.10.clone
  0.1 0.7 multiply_add_fusion.1
  0.8 0.9 convert_reduce_fusion.1
  1.8 0.7 fusion.14
  2.5 0.1 multiply_reduce_fusion
  2.6 0.1 tile.10
  2.7 0.6 compare_select_fusion.2.top_idx
  3.3 0.7 iota_add_fusion
  4.0 0.1 convert_reduce_fusion
  4.1 0.1 select_reduce_fusion
  4.2 0.1 copy.29
  4.3 0.1 copy.31
  4.4 0.7 add_add_fusion.near
  5.1 0.1 sub.69
  5.3 0.7 pad.4.blk_src
  5.9 1.0 pad_maximum_fusion
  6.9 1.3 %reshape.175.transfers = bf16[2336,32]{1,0:T(8,128)(2,1)} reshape(bf16[73,1024]{1,0:T(8,128)(2,1)S(1)} %pad_maximum_fusion) | data formatting | bytes 299008 | tf_op jit(solution)/shard_map/reshape | solution.py:556
  8.2 0.0 copy-done
  8.2 0.4 convolution_convert_fusion
  8.6 1.0 reshape.172.blk
  9.6 0.0 copy-done.1
  9.6 0.9 copy.36
  10.5 63.2 %exchange.1 = (bf16[16,8,16,128]{3,2,1,0:T(8,128)(2,1)}, s32[16,8,1,128]{3,2,1,0:T(1,128)}, bf16[2,16,4,32,128]{4,3,2,1,0:T(8,128)(2,1)}, bf16[16,32,128]{2,1,0:...) custom-call(s32[64,30]{1,0:T(8,128)} %add_add_fusion.near, ...), custom_call_target="tpu_custom_call" | custom-call | flops 1000000000 | bytes 10000000 | tf_op jit(solution)/shard_map/exchange/pallas_call | solution.py:300
  73.8 1.0 slice_reduce_fusion
  74.8 0.1 eq.125
  74.9 1.0 reshape.179
  75.9 0.2 copy.38
  76.0 0.1 reshape.180
  76.2 0.6 subtract_convert_fusion.1
  76.8 1.3 %reshape.176 = bf16[256,1024]{1,0:T(8,128)(2,1)S(1)} reshape(bf16[16,8,16,128]{3,2,1,0:T(8,128)(2,1)} %get-tuple-element.21) | data formatting | bytes 1048576 | tf_op jit(solution)/shard_map/reshape | solution.py:563
  78.1 0.2 copy.33
  78.3 0.3 convolution_bitcast_fusion
  78.6 0.6 copy.34
  79.2 1.0 reshape.177
  80.2 0.8 subtract_convert_fusion
  81.0 28.2 %near.1 = bf16[8192,128]{1,0:T(8,128)(2,1)} custom-call(s32[64,30]{1,0:T(8,128)} %add_add_fusion.near, bf16[200,32,128]{2,1,0:T(8,128)(2,1)} %get-tuple-element.15.source, bf16[64,128,32]{2,1,0:T(8,128)(2,1)} %get-tuple-element.16.target, bf16[64,128,128]{2,1,0:T(8,128)(2,1)} %bitcast.25, bf16[64,128,128]{2,1,0:T(8,128)(2,1)} %get-tuple-element.17.partner, ...), custom_call_target="tpu_custom_call" | custom-call | flops 5000000000 | bytes 10000000 | tf_op jit(solution)/shard_map/near/pallas_call | solution.py:492
  (5 shorter events, 0.0 us)
Async XLA Ops:
  0.0 8.2 %copy-start = (bf16[189,1024]{1,0:T(8,128)(2,1)S(1)}, bf16[189,1024]{1,0:T(8,128)(2,1)}, u32[]{:S(2)}) copy-start(bf16[189,1024]{1,0:T(8,128)(2,1)} %param.20) | copy-start | bytes 1161220
  0.0 9.6 %copy-start.1 = (bf16[64,4096]{1,0:T(8,128)(2,1)S(1)}, bf16[64,4096]{1,0:T(8,128)(2,1)}, u32[]{:S(2)}) copy-start(bf16[64,4096]{1,0:T(8,128)(2,1)} %param.16) | copy-start | bytes 1572868
where the time goes:
time: 112 us; the launch traced here: 109 us
  Pallas kernels  91.4 us (82%)
  local copies, waits for them, and re-layouts  9.76 us (9%)
  other arithmetic  7.16 us (6%)
    pallas_call x1, Pallas kernels, exchange_call(): pl.pallas_call(functools.partial(exchange_kernel, math.sqrt(NNEAR * M)),...  63.2 us
    pallas_call x1, Pallas kernels, near_call(): pl.pallas_call(near_kernel, grid_spec=grid_spec, out_shape=jax.ShapeDtype...  28.2 us

commit v1 on v0

--- a/solution.py
+++ b/solution.py
@@ -124,21 +124,6 @@
             points[i, l : l + 1, :] = coords[i : i + 1, l * M : (l + 1) * M]
     pool[2 * LEAVES] = jnp.zeros((M, RHS), bf16)
 
-    fetch.wait()
-
-    def one_mid(m, c):
-        rows = []
-        for b in range(GROUP):
-            rows.append(dot(basis[m * GROUP + b], pool[m * GROUP + b]).astype(bf16))
-        first = pl.multiple_of(m * GROUP * K, GROUP * K)
-        rows = dot_t(transfers[pl.ds(first, GROUP * K), :], jnp.concatenate(rows, axis=0))
-        mids[pl.ds(pl.multiple_of(m * K, K), K), :] = rows.astype(bf16)
-        return c
-
-    lax.fori_loop(0, GROUP, one_mid, 0)
-    base = dot_t(transfers[LEAVES * K : LEAVES * K + GROUP * K, :], mids[...]).astype(bf16)
-    coeffs[0] = base
-    coeffs[1] = dot_t(transfers[LEAVES * K + GROUP * K :, :], base).astype(bf16)
     pl.semaphore_wait(barrier, len(greeted))
 
     def remote(src, dst, k, to):
@@ -156,11 +141,6 @@
         whole.wait_send()
         whole.wait_recv()
 
-    for o in range(1, 4):
-        to = plane * GROUP + lax.rem(y + o, 4) * 2 + core
-        remote(coeffs.at[0], every.at[core, plane, y], 6, to).start()
-    for to in peers:
-        remote(coeffs.at[1], lifted.at[place], 7, to).start()
     for to in peers:
         remote(blk.at[to % GROUP], half.at[place], 4, to).start()
         remote(blk_src.at[to % GROUP], half_src.at[place], 5, to).start()
@@ -168,14 +148,37 @@
     to_other = remote(points, others.at[1], 1, next_chip)
     to_partner.start()
     to_other.start()
-    swap = remote(held, pool.at[pl.ds(LEAVES, LEAVES)], 12, across_chip)
+    swap = remote(charges, pool.at[pl.ds(LEAVES, LEAVES)], 12, across_chip)
     swap.start()
     for p in planes:
         to = p * GROUP + place
         remote(top, r_top.at[plane], 2, to).start()
         remote(top_idx, r_idx.at[plane], 3, to).start()
-    outward = remote(held, other, 13, next_chip)
-    outward.start()
+    piece = pl.ds(0, 16)
+    remote(charges.at[piece], other.at[piece], 13, next_chip).start()
+
+    fetch.wait()
+
+    def one_mid(m, c):
+        rows = []
+        for b in range(GROUP):
+            rows.append(dot(basis[m * GROUP + b], pool[m * GROUP + b]).astype(bf16))
+        first = pl.multiple_of(m * GROUP * K, GROUP * K)
+        rows = dot_t(transfers[pl.ds(first, GROUP * K), :], jnp.concatenate(rows, axis=0))
+        mids[pl.ds(pl.multiple_of(m * K, K), K), :] = rows.astype(bf16)
+        return c
+
+    lax.fori_loop(0, GROUP, one_mid, 0)
+    base = dot_t(transfers[LEAVES * K : LEAVES * K + GROUP * K, :], mids[...]).astype(bf16)
+    coeffs[0] = base
+    coeffs[1] = dot_t(transfers[LEAVES * K + GROUP * K :, :], base).astype(bf16)
+    for o in range(1, 4):
+        to = plane * GROUP + lax.rem(y + o, 4) * 2 + core
+        remote(coeffs.at[0], every.at[core, plane, y], 6, to).start()
+    for to in peers:
+        remote(coeffs.at[1], lifted.at[place], 7, to).start()
+    piece = pl.ds(16, LEAVES - 16)
+    remote(charges.at[piece], other.at[piece], 13, next_chip).start()
     own = [
         pltpu.make_async_copy(blk.at[place], half.at[place], local.at[1]),
         pltpu.make_async_copy(blk_src.at[place], half_src.at[place], local.at[2]),
@@ -196,7 +199,7 @@
         return lines[pl.ds(pl.multiple_of(l * K, K), K), :]
 
     def put_target(l, c):
-        target[l] = line(l).T.astype(bf16)
+        target[l] = line(l).astype(bf16)
         return c
 
     def put_source(block):
@@ -250,15 +253,20 @@
     def close_group(group, c):
         for b in range(GROUP):
             leaf = group * GROUP + b
+            mine_t = target[leaf].T
             for j in range(HALF // 2):
                 one, two = near[leaf, 2 * j], near[leaf, 2 * j + 1]
-                pair_rows(
-                    b, target[leaf], one, two, j, source, pool, kern, gathered, 2 * LEAVES
-                )
+                kernel_rows(b, mine_t, one, two, j, source, kern)
+                charge_rows(b, one, two, j, pool, gathered, 2 * LEAVES)
             sums[leaf] = dot(kern[b], gathered[b])
         return c
 
-    lax.fori_loop(0, 2, close_group, 0)
+    def close_half(k):
+        lax.fori_loop(2 * k, 2 * k + 2, close_group, 0)
+        done = pl.ds(2 * k * GROUP, 2 * GROUP)
+        pltpu.make_async_copy(sums.at[done], partial.at[done], leave).start()
+
+    close_half(0)
 
     finish(r_top.at[pl.ds(0, 15)], 2)
     finish(r_idx.at[pl.ds(0, 15)], 3)
@@ -271,17 +279,16 @@
     own_part = pltpu.make_async_copy(part, tops.at[place], local.at[0])
     own_part.start()
 
-    lax.fori_loop(2, 4, close_group, 0)
+    close_half(1)
     finish(every.at[0, pl.ds(0, 15)], 8)
     across = remote(every.at[core], every.at[core], 11, across_chip)
     across.start()
-    lax.fori_loop(4, 6, close_group, 0)
+    close_half(2)
     own_part.wait()
     finish(tops.at[pl.ds(0, GROUP - 1)], 10)
     top_sum[...] = jnp.sum(tops[...].astype(f32), axis=0)
-    lax.fori_loop(6, GROUP, close_group, 0)
+    close_half(3)
     away = pltpu.make_async_copy(sums, partial, leave)
-    away.start()
     finish(top_all.at[pl.ds(0, 15)], 9)
     across.wait()
     for copy in own:
@@ -290,7 +297,7 @@
     finish(r_src.at[pl.ds(0, 15)], 15)
     keep.wait()
     away.wait()
-    outward.wait()
+    finish(other, 13)
 
 
 def exchange_call(near, blk, blk_src, top, top_idx, coords, charges, basis, transfers):
@@ -306,7 +313,7 @@
             shape((16, K, RHS), bf16),
             shape((16, K * K), f32),
             shape((POOL + 8, K, M), bf16),
-            shape((LEAVES, M, K), bf16),
+            shape((LEAVES, K, M), bf16),
             shape((LEAVES, M, RHS), bf16),
             shape((LEAVES, M, RHS), bf16),
             shape((LEAVES, M, RHS), f32),
@@ -350,9 +357,12 @@
     )(near, blk, blk_src, top, top_idx, coords, charges, basis, transfers)
 
 
-def pair_rows(slot, mine, one, two, j, source, pool, kern, gathered, last):
+def kernel_rows(slot, mine, one, two, j, source, kern):
     squares = dot(mine, jnp.concatenate([source[one], source[two]], axis=1))
     kern[slot, :, 2 * M * j : 2 * M * (j + 1)] = lax.rsqrt(squares.astype(bf16))
+
+
+def charge_rows(slot, one, two, j, pool, gathered, last):
     gathered[slot, 2 * M * j : 2 * M * j + M] = pool[jnp.minimum(one, last)]
     gathered[slot, 2 * M * j + M : 2 * M * (j + 1)] = pool[jnp.minimum(two, last)]
 
@@ -394,9 +404,23 @@
 ):
     step = pl.program_id(0)
 
+    def entries(b):
+        leaf = step * GROUP + b
+        return [
+            (near[leaf, HALF + 2 * j], near[leaf, HALF + 2 * j + 1], j)
+            for j in range(HALF // 2)
+        ]
+
+    def fill(b):
+        mine = target[b].T
+        for one, two, j in entries(b):
+            kernel_rows(b, mine, one, two, j, source, kern)
+
     @pl.when(step == 0)
     def _():
         copies = load_pool((here, partner, other), pool, sems)
+        for b in range(GROUP):
+            fill(b)
         extra[...] = jnp.zeros_like(extra)
         top_field = (dot(t_high[...], top_all[...]) + dot(t_low[...], top_all[...])).astype(bf16)
         coupled = dot(a_high[...], every[...]) + dot(a_low[...], every[...])
@@ -419,7 +443,7 @@
 
             def one_entry(e, total):
                 g = near[leaf, e]
-                squares = dot(target[b], source[g])
+                squares = dot_t(target[b], source[g])
                 return total + dot(lax.rsqrt(squares.astype(bf16)), pool[g])
 
             extra[b] = lax.fori_loop(
@@ -429,18 +453,22 @@
 
         lax.fori_loop(0, GROUP, one_leaf, 0)
 
-    down = transfers[pl.ds(pl.multiple_of((LEAVES + step) * K, K), K), :]
-    mid = dot(down, base[...]).astype(bf16)
-    down = transfers[pl.ds(pl.multiple_of(step * GROUP * K, GROUP * K), GROUP * K), :]
-    fields = dot(down, mid).astype(bf16)
-    for b in range(GROUP):
-        leaf = step * GROUP + b
-        for j in range(HALF // 2):
-            one, two = near[leaf, HALF + 2 * j], near[leaf, HALF + 2 * j + 1]
-            pair_rows(b, target[b], one, two, j, source, pool, kern, gathered, POOL)
-        far = dot_t(basis[b], fields[b * K : (b + 1) * K])
-        total = dot(kern[b], gathered[b]) + far + (partial[b] + extra[b])
-        out[pl.ds(b * M, M), :] = total.astype(bf16)
+    def group(filled):
+        down = transfers[pl.ds(pl.multiple_of((LEAVES + step) * K, K), K), :]
+        mid = dot(down, base[...]).astype(bf16)
+        down = transfers[pl.ds(pl.multiple_of(step * GROUP * K, GROUP * K), GROUP * K), :]
+        fields = dot(down, mid).astype(bf16)
+        for b in range(GROUP):
+            if not filled:
+                fill(b)
+            for one, two, j in entries(b):
+                charge_rows(b, one, two, j, pool, gathered, POOL)
+            far = dot_t(basis[b], fields[b * K : (b + 1) * K])
+            total = dot(kern[b], gathered[b]) + far + (partial[b] + extra[b])
+            out[pl.ds(b * M, M), :] = total.astype(bf16)
+
+    pl.when(step == 0)(lambda: group(True))
+    pl.when(step > 0)(lambda: group(False))
 
     @pl.when(late > 0)
     def _():
@@ -472,7 +500,7 @@
         grid=(LEAVES // GROUP,),
         in_specs=[
             vmem(*source.shape),
-            pl.BlockSpec((GROUP, M, K), lambda i, _: (i, 0, 0)),
+            pl.BlockSpec((GROUP, K, M), lambda i, _: (i, 0, 0)),
             anywhere,
             anywhere,
             anywhere,

time: 112 us -> 115 us (1.027)
  the two profiles are of different devices: /device:TPU:102 before, /device:TPU:1 now
where the time goes in v1:
time: 115 us
  Pallas kernels  97.1 us (84%)
  local copies, waits for them, and re-layouts  9.76 us (8%)
  other arithmetic  7.17 us (6%)
    pallas_call x1, Pallas kernels, exchange_call(): pl.pallas_call(functools.partial(exchange_kernel, math.sqrt(NNEAR * M)),...  68.5 us
    pallas_call x1, Pallas kernels, near_call(): pl.pallas_call(near_kernel, grid_spec=grid_spec, out_shape=jax.ShapeDtype...  28.6 us

profile of v1, /device:TPU:1, one launch (start us, length us, event | category | flops | bytes accessed | tf_op | source)
XLA Modules:
  0.0 115.1 jit_solution(11508125886134246480)
XLA Ops:
  0.0 0.0 copy-start
  0.0 0.0 copy-start.1
  0.0 0.1 pad.10.clone
  0.1 0.7 multiply_add_fusion.1
  0.8 0.9 convert_reduce_fusion.1
  1.8 0.7 fusion.14
  2.5 0.1 multiply_reduce_fusion
  2.6 0.1 tile.10
  2.7 0.5 compare_select_fusion.2.top_idx
  3.2 0.7 iota_add_fusion
  4.0 0.1 convert_reduce_fusion
  4.1 0.1 select_reduce_fusion
  4.2 0.1 copy.29
  4.3 0.1 copy.31
  4.4 0.7 add_add_fusion.near
  5.1 0.1 sub.69
  5.2 0.7 pad.4.blk_src
  5.9 1.0 pad_maximum_fusion
  6.9 1.2 %reshape.175.transfers = bf16[2336,32]{1,0:T(8,128)(2,1)} reshape(bf16[73,1024]{1,0:T(8,128)(2,1)S(1)} %pad_maximum_fusion) | data formatting | bytes 299008 | tf_op jit(solution)/shard_map/reshape | solution.py:584
  8.1 0.0 copy-done
  8.1 0.4 convolution_convert_fusion
  8.5 1.0 reshape.172.blk
  9.6 0.0 copy-done.1
  9.6 0.9 copy.36
  10.5 68.5 %exchange.1 = (bf16[16,8,16,128]{3,2,1,0:T(8,128)(2,1)}, s32[16,8,1,128]{3,2,1,0:T(1,128)}, bf16[2,16,4,32,128]{4,3,2,1,0:T(8,128)(2,1)}, bf16[16,32,128]{2,1,0:...) custom-call(s32[64,30]{1,0:T(8,128)} %add_add_fusion.near, ...), custom_call_target="tpu_custom_call" | custom-call | flops 1000000000 | bytes 10000000 | tf_op jit(solution)/shard_map/exchange/pallas_call | solution.py:307
  79.0 1.0 slice_reduce_fusion
  80.0 0.1 eq.125
  80.2 1.0 reshape.179
  81.1 0.2 copy.38
  81.3 0.1 reshape.180
  81.4 0.6 subtract_convert_fusion.1
  82.1 1.3 %reshape.176 = bf16[256,1024]{1,0:T(8,128)(2,1)S(1)} reshape(bf16[16,8,16,128]{3,2,1,0:T(8,128)(2,1)} %get-tuple-element.21) | data formatting | bytes 1048576 | tf_op jit(solution)/shard_map/reshape | solution.py:591
  83.3 0.2 copy.33
  83.5 0.3 convolution_bitcast_fusion
  83.8 0.6 copy.34
  84.5 1.0 reshape.177
  85.4 0.9 subtract_convert_fusion
  86.3 28.6 %near.1 = bf16[8192,128]{1,0:T(8,128)(2,1)} custom-call(s32[64,30]{1,0:T(8,128)} %add_add_fusion.near, bf16[200,32,128]{2,1,0:T(8,128)(2,1)} %get-tuple-element.15.source, bf16[64,32,128]{2,1,0:T(8,128)(2,1)} %get-tuple-element.16.target, bf16[64,128,128]{2,1,0:T(8,128)(2,1)} %bitcast.28, bf16[64,128,128]{2,1,0:T(8,128)(2,1)} %get-tuple-element.17.partner, ...), custom_call_target="tpu_custom_call" | custom-call | flops 5000000000 | bytes 10000000 | tf_op jit(solution)/shard_map/near/pallas_call | solution.py:520
  (5 shorter events, 0.0 us)
Async XLA Ops:
  0.0 8.1 %copy-start = (bf16[189,1024]{1,0:T(8,128)(2,1)S(1)}, bf16[189,1024]{1,0:T(8,128)(2,1)}, u32[]{:S(2)}) copy-start(bf16[189,1024]{1,0:T(8,128)(2,1)} %param.20) | copy-start | bytes 1161220
  0.0 9.6 %copy-start.1 = (bf16[64,4096]{1,0:T(8,128)(2,1)S(1)}, bf16[64,4096]{1,0:T(8,128)(2,1)}, u32[]{:S(2)}) copy-start(bf16[64,4096]{1,0:T(8,128)(2,1)} %param.16) | copy-start | bytes 1572868

commit v2 on v1

--- a/solution.py
+++ b/solution.py
@@ -64,7 +64,6 @@
 
 def exchange_kernel(
     scale,
-    near,
     blk,
     blk_src,
     top,
@@ -81,12 +80,7 @@
     source,
     target,
     partner,
-    other,
-    partial,
-    pool,
-    kern,
-    gathered,
-    sums,
+    held,
     points,
     half,
     half_src,
@@ -103,12 +97,10 @@
     send,
     recv,
     local,
-    leave,
 ):
     me = lax.axis_index(AXIS)
     plane, place = me // GROUP, me % GROUP
     core, y = place % 2, place // 2
-    held = pool.at[pl.ds(0, LEAVES)]
     fetch = pltpu.make_async_copy(charges, held, local.at[0])
     fetch.start()
     barrier = pltpu.get_barrier_semaphore()
@@ -122,8 +114,22 @@
     for i in range(3):
         for l in range(LEAVES):
             points[i, l : l + 1, :] = coords[i : i + 1, l * M : (l + 1) * M]
-    pool[2 * LEAVES] = jnp.zeros((M, RHS), bf16)
-
+
+    fetch.wait()
+
+    def one_mid(m, c):
+        rows = []
+        for b in range(GROUP):
+            rows.append(dot(basis[m * GROUP + b], held[m * GROUP + b]).astype(bf16))
+        first = pl.multiple_of(m * GROUP * K, GROUP * K)
+        rows = dot_t(transfers[pl.ds(first, GROUP * K), :], jnp.concatenate(rows, axis=0))
+        mids[pl.ds(pl.multiple_of(m * K, K), K), :] = rows.astype(bf16)
+        return c
+
+    lax.fori_loop(0, GROUP, one_mid, 0)
+    base = dot_t(transfers[LEAVES * K : LEAVES * K + GROUP * K, :], mids[...]).astype(bf16)
+    coeffs[0] = base
+    coeffs[1] = dot_t(transfers[LEAVES * K + GROUP * K :, :], base).astype(bf16)
     pl.semaphore_wait(barrier, len(greeted))
 
     def remote(src, dst, k, to):
@@ -141,6 +147,11 @@
         whole.wait_send()
         whole.wait_recv()
 
+    for o in range(1, 4):
+        to = plane * GROUP + lax.rem(y + o, 4) * 2 + core
+        remote(coeffs.at[0], every.at[core, plane, y], 6, to).start()
+    for to in peers:
+        remote(coeffs.at[1], lifted.at[place], 7, to).start()
     for to in peers:
         remote(blk.at[to % GROUP], half.at[place], 4, to).start()
         remote(blk_src.at[to % GROUP], half_src.at[place], 5, to).start()
@@ -148,37 +159,12 @@
     to_other = remote(points, others.at[1], 1, next_chip)
     to_partner.start()
     to_other.start()
-    swap = remote(charges, pool.at[pl.ds(LEAVES, LEAVES)], 12, across_chip)
+    swap = remote(held, partner, 12, across_chip)
     swap.start()
     for p in planes:
         to = p * GROUP + place
         remote(top, r_top.at[plane], 2, to).start()
         remote(top_idx, r_idx.at[plane], 3, to).start()
-    piece = pl.ds(0, 16)
-    remote(charges.at[piece], other.at[piece], 13, next_chip).start()
-
-    fetch.wait()
-
-    def one_mid(m, c):
-        rows = []
-        for b in range(GROUP):
-            rows.append(dot(basis[m * GROUP + b], pool[m * GROUP + b]).astype(bf16))
-        first = pl.multiple_of(m * GROUP * K, GROUP * K)
-        rows = dot_t(transfers[pl.ds(first, GROUP * K), :], jnp.concatenate(rows, axis=0))
-        mids[pl.ds(pl.multiple_of(m * K, K), K), :] = rows.astype(bf16)
-        return c
-
-    lax.fori_loop(0, GROUP, one_mid, 0)
-    base = dot_t(transfers[LEAVES * K : LEAVES * K + GROUP * K, :], mids[...]).astype(bf16)
-    coeffs[0] = base
-    coeffs[1] = dot_t(transfers[LEAVES * K + GROUP * K :, :], base).astype(bf16)
-    for o in range(1, 4):
-        to = plane * GROUP + lax.rem(y + o, 4) * 2 + core
-        remote(coeffs.at[0], every.at[core, plane, y], 6, to).start()
-    for to in peers:
-        remote(coeffs.at[1], lifted.at[place], 7, to).start()
-    piece = pl.ds(16, LEAVES - 16)
-    remote(charges.at[piece], other.at[piece], 13, next_chip).start()
     own = [
         pltpu.make_async_copy(blk.at[place], half.at[place], local.at[1]),
         pltpu.make_async_copy(blk_src.at[place], half_src.at[place], local.at[2]),
@@ -246,28 +232,6 @@
     for i in range(2):
         side(features(scale, [others[i, j] for j in range(3)], False), put_source(i + 1), LEAVES)
 
-    swap.wait()
-    keep = pltpu.make_async_copy(pool.at[pl.ds(LEAVES, LEAVES)], partner, local.at[1])
-    keep.start()
-
-    def close_group(group, c):
-        for b in range(GROUP):
-            leaf = group * GROUP + b
-            mine_t = target[leaf].T
-            for j in range(HALF // 2):
-                one, two = near[leaf, 2 * j], near[leaf, 2 * j + 1]
-                kernel_rows(b, mine_t, one, two, j, source, kern)
-                charge_rows(b, one, two, j, pool, gathered, 2 * LEAVES)
-            sums[leaf] = dot(kern[b], gathered[b])
-        return c
-
-    def close_half(k):
-        lax.fori_loop(2 * k, 2 * k + 2, close_group, 0)
-        done = pl.ds(2 * k * GROUP, 2 * GROUP)
-        pltpu.make_async_copy(sums.at[done], partial.at[done], leave).start()
-
-    close_half(0)
-
     finish(r_top.at[pl.ds(0, 15)], 2)
     finish(r_idx.at[pl.ds(0, 15)], 3)
     named = jnp.sum(r_idx[...], axis=0)
@@ -279,28 +243,22 @@
     own_part = pltpu.make_async_copy(part, tops.at[place], local.at[0])
     own_part.start()
 
-    close_half(1)
     finish(every.at[0, pl.ds(0, 15)], 8)
     across = remote(every.at[core], every.at[core], 11, across_chip)
     across.start()
-    close_half(2)
     own_part.wait()
     finish(tops.at[pl.ds(0, GROUP - 1)], 10)
     top_sum[...] = jnp.sum(tops[...].astype(f32), axis=0)
-    close_half(3)
-    away = pltpu.make_async_copy(sums, partial, leave)
     finish(top_all.at[pl.ds(0, 15)], 9)
     across.wait()
     for copy in own:
         copy.wait()
     finish(r_blk.at[pl.ds(0, 15)], 14)
     finish(r_src.at[pl.ds(0, 15)], 15)
-    keep.wait()
-    away.wait()
-    finish(other, 13)
-
-
-def exchange_call(near, blk, blk_src, top, top_idx, coords, charges, basis, transfers):
+    swap.wait()
+
+
+def exchange_call(blk, blk_src, top, top_idx, coords, charges, basis, transfers):
     inside = pl.BlockSpec(memory_space=pltpu.VMEM)
     anywhere = pl.BlockSpec(memory_space=pl.ANY)
     shape = jax.ShapeDtypeStruct
@@ -315,22 +273,16 @@
             shape((POOL + 8, K, M), bf16),
             shape((LEAVES, K, M), bf16),
             shape((LEAVES, M, RHS), bf16),
-            shape((LEAVES, M, RHS), bf16),
-            shape((LEAVES, M, RHS), f32),
         ),
         in_specs=[
-            pl.BlockSpec(memory_space=pltpu.SMEM),
             *[inside] * 5,
             anywhere,
             inside,
             inside,
         ],
-        out_specs=(*[inside] * 7, *[anywhere] * 3),
+        out_specs=(*[inside] * 7, anywhere),
         scratch_shapes=[
-            pltpu.VMEM((2 * LEAVES + 1, M, RHS), bf16),
-            pltpu.VMEM((GROUP, M, M * HALF), bf16),
-            pltpu.VMEM((GROUP, M * HALF, RHS), bf16),
-            pltpu.VMEM((LEAVES, M, RHS), f32),
+            pltpu.VMEM((LEAVES, M, RHS), bf16),
             pltpu.VMEM((3, LEAVES, M), f32),
             pltpu.VMEM(blk.shape, bf16),
             pltpu.VMEM(blk_src.shape, jnp.int32),
@@ -347,14 +299,13 @@
             pltpu.SemaphoreType.DMA((16,)),
             pltpu.SemaphoreType.DMA((16,)),
             pltpu.SemaphoreType.DMA((7,)),
-            pltpu.SemaphoreType.DMA,
         ],
         compiler_params=pltpu.CompilerParams(
             collective_id=0, has_side_effects=True, vmem_limit_bytes=63 * 1024 * 1024
         ),
         cost_estimate=pl.CostEstimate(flops=10**9, bytes_accessed=10**7, transcendentals=0),
         name="exchange",
-    )(near, blk, blk_src, top, top_idx, coords, charges, basis, transfers)
+    )(blk, blk_src, top, top_idx, coords, charges, basis, transfers)
 
 
 def kernel_rows(slot, mine, one, two, j, source, kern):
@@ -367,15 +318,47 @@
     gathered[slot, 2 * M * j + M : 2 * M * (j + 1)] = pool[jnp.minimum(two, last)]
 
 
-def load_pool(refs, pool, sems):
+def load_pool(refs, pool, sems, last):
     copies = [
         pltpu.make_async_copy(ref, pool.at[pl.ds(LEAVES * i, LEAVES)], sems.at[i])
         for i, ref in enumerate(refs)
     ]
     for copy in copies:
         copy.start()
-    pool[POOL] = jnp.zeros((M, RHS), bf16)
+    pool[last] = jnp.zeros((M, RHS), bf16)
     return copies
+
+
+def close_kernel(near, source, target, here, partner, out, pool, kern, gathered, sems):
+    step = pl.program_id(0)
+
+    def entries(b):
+        leaf = step * GROUP + b
+        return [(near[leaf, 2 * j], near[leaf, 2 * j + 1], j) for j in range(HALF // 2)]
+
+    def fill(b):
+        mine = target[b].T
+        for one, two, j in entries(b):
+            kernel_rows(b, mine, one, two, j, source, kern)
+
+    def group(filled):
+        for b in range(GROUP):
+            if not filled:
+                fill(b)
+            for one, two, j in entries(b):
+                charge_rows(b, one, two, j, pool, gathered, 2 * LEAVES)
+            out[b] = dot(kern[b], gathered[b])
+
+    @pl.when(step == 0)
+    def _():
+        copies = load_pool((here, partner), pool, sems, 2 * LEAVES)
+        for b in range(GROUP):
+            fill(b)
+        for copy in copies:
+            copy.wait()
+        group(True)
+
+    pl.when(step > 0)(lambda: group(False))
 
 
 def near_kernel(
@@ -418,7 +401,7 @@
 
     @pl.when(step == 0)
     def _():
-        copies = load_pool((here, partner, other), pool, sems)
+        copies = load_pool((here, partner, other), pool, sems, POOL)
         for b in range(GROUP):
             fill(b)
         extra[...] = jnp.zeros_like(extra)
@@ -427,10 +410,6 @@
         base[...] = (coupled + dot(transfers[(LEAVES + GROUP) * K :, :], top_field)).astype(bf16)
         for copy in copies:
             copy.wait()
-
-        @pl.when(near[0, 2 * HALF + 1] > 0)
-        def _():
-            pool[pl.ds(2 * LEAVES, LEAVES)] = jnp.zeros((LEAVES, M, RHS), bf16)
 
     late = jnp.int32(0)
     for b in range(GROUP):
@@ -475,9 +454,9 @@
         extra[...] = jnp.zeros_like(extra)
 
 
-def near_scratch():
+def near_scratch(leaves):
     return [
-        pltpu.VMEM((POOL + 1, M, RHS), bf16),
+        pltpu.VMEM((leaves, M, RHS), bf16),
         pltpu.VMEM((GROUP, M, M * HALF), bf16),
         pltpu.VMEM((GROUP, M * HALF, RHS), bf16),
     ]
@@ -491,6 +470,29 @@
         flops=5 * 10**9, bytes_accessed=10**7, transcendentals=10**7
     ),
 )
+
+
+def close_call(near, source, target, here, partner):
+    anywhere = pl.BlockSpec(memory_space=pl.ANY)
+    grid_spec = pltpu.PrefetchScalarGridSpec(
+        num_scalar_prefetch=1,
+        grid=(LEAVES // GROUP,),
+        in_specs=[
+            vmem(*source.shape),
+            pl.BlockSpec((GROUP, K, M), lambda i, _: (i, 0, 0)),
+            anywhere,
+            anywhere,
+        ],
+        out_specs=pl.BlockSpec((GROUP, M, RHS), lambda i, _: (i, 0, 0)),
+        scratch_shapes=[*near_scratch(2 * LEAVES + 1), pltpu.SemaphoreType.DMA((2,))],
+    )
+    return pl.pallas_call(
+        close_kernel,
+        grid_spec=grid_spec,
+        out_shape=jax.ShapeDtypeStruct((LEAVES, M, RHS), f32),
+        name="close",
+        **NEAR_PARAMS,
+    )(near, source, target, here, partner)
 
 
 def near_call(near, source, target, here, partner, other, partial, far, transfers, basis):
@@ -511,7 +513,7 @@
         ],
         out_specs=pl.BlockSpec((GROUP * M, RHS), lambda i, _: (i, 0)),
         scratch_shapes=[
-            *near_scratch(),
+            *near_scratch(POOL + 1),
             pltpu.VMEM((K, RHS), bf16),
             pltpu.VMEM((GROUP, M, RHS), f32),
             pltpu.SemaphoreType.DMA((3,)),
@@ -526,7 +528,7 @@
     )(near, source, target, here, partner, other, partial, *far, transfers, basis)
 
 
-def near_lists(near_leaves, core, edge):
+def near_lists(near_leaves, core):
     block, inside = near_leaves // LEAVES, near_leaves % LEAVES
     moved = jnp.where(block == 1, 0, jnp.where((block == 0) == (core == 0), 2, 1))
     place = moved * LEAVES + inside
@@ -539,7 +541,7 @@
     )
     ordered = jnp.where(ordered == 0, POOL, ordered - 1)
     ready = jnp.minimum(NNEAR - jnp.sum(away, axis=1, keepdims=True), HALF)
-    return jnp.concatenate([ordered, ready, jnp.full_like(ready, edge)], axis=1)
+    return jnp.concatenate([ordered, ready], axis=1)
 
 
 def high_low(v):
@@ -582,11 +584,14 @@
     basis = leaf_basis.reshape(LEAVES, K, M)
     transfers = jnp.concatenate([leaf_transfer, mid_transfer, base_transfer], axis=0)
     transfers = transfers.reshape((LEAVES + GROUP + 1) * K, K)
-    edge = ((me == 0) | (me == N - 1)).astype(jnp.int32)
-    near = near_lists(near_leaves, me % 2, edge)
-    r_blk, r_src, every, top_all, t, source, target, partner, other, partial = exchange_call(
-        near, blk, blk_src, top_coupling, top_idx, coords, rows, basis, transfers
-    )
+    r_blk, r_src, every, top_all, t, source, target, partner = exchange_call(
+        blk, blk_src, top_coupling, top_idx, coords, rows, basis, transfers
+    )
+    outward = [(i, i + 1) for i in range(1, N - 1, 2)] + [(i, i - 1) for i in range(2, N, 2)]
+    sent, partner, listed = lax.optimization_barrier((rows, partner, near_leaves))
+    other = lax.ppermute(sent, AXIS, outward)
+    near = near_lists(listed, me % 2)
+    partial = close_call(near, source, target, rows, partner)
     by_source = (lane[:, None] == r_src[:, :, 0, :2].reshape(1, 2 * N)).astype(bf16)
     a = dot(by_source, r_blk.reshape(2 * N, K * K))
     a = a.reshape(N, K, K).transpose(1, 0, 2).reshape(K, N * K)

time: 115 us -> 108 us (0.939)
  the two profiles are of different devices: /device:TPU:1 before, /device:TPU:32 now
where the time goes in v2:
time: 108 us; the launch traced here: 106 us
  Pallas kernels  80.3 us (74%)
  local copies, waits for them, and re-layouts  10.9 us (10%)
  starting transfers between devices  6.8 us (6%)
  other arithmetic  6.41 us (6%)
    pallas_call x1, Pallas kernels, exchange_call(): pl.pallas_call(functools.partial(exchange_kernel, math.sqrt(NNEAR * M)),...  29.1 us
    pallas_call x1, Pallas kernels, near_call(): pl.pallas_call(near_kernel, grid_spec=grid_spec, out_shape=jax.ShapeDtype...  27.7 us
    pallas_call x1, Pallas kernels, close_call(): pl.pallas_call(close_kernel, grid_spec=grid_spec, out_shape=jax.ShapeDtyp...  23.5 us
    ppermute x1, starting transfers between devices, per_device(): other = lax.ppermute(sent, AXIS, outward)  6.8 us
  transfers between devices with their start and end apart: 1, of which 0 were waited for; matrix products, arithmetic and copies ran while one was open for 9% of the time, Pallas kernels for 22%

profile of v2, /device:TPU:32, one launch (start us, length us, event | category | flops | bytes accessed | tf_op | source)
XLA Modules:
  0.0 105.5 jit_solution(12693391539970511048)
XLA Ops:
  0.0 0.0 copy-start
  0.0 0.0 copy-start.1
  0.0 1.0 convert_reduce_fusion.1
  1.0 0.7 fusion.14
  1.7 0.1 multiply_reduce_fusion
  1.8 0.7 multiply_add_fusion.1
  2.5 0.1 tile.10
  2.6 0.1 sub.65
  2.7 0.7 pad.4.blk_src
  3.4 1.0 pad_maximum_fusion
  4.4 1.2 %reshape.175.transfers = bf16[2336,32]{1,0:T(8,128)(2,1)} reshape(bf16[73,1024]{1,0:T(8,128)(2,1)S(1)} %pad_maximum_fusion) | data formatting | bytes 299008 | tf_op jit(solution)/shard_map/reshape | solution.py:586
  5.6 0.0 copy-done
  5.6 0.4 convolution_convert_fusion
  6.0 1.0 reshape.173.blk
  7.1 0.0 copy-done.1
  7.1 0.9 copy.36
  8.0 0.0 copy-start.4
  8.0 0.5 compare_select_fusion.2.top_idx
  8.5 29.1 %exchange.1 = (bf16[16,8,16,128]{3,2,1,0:T(8,128)(2,1)}, s32[16,8,1,128]{3,2,1,0:T(1,128)}, bf16[2,16,4,32,128]{4,3,2,1,0:T(8,128)(2,1)}, bf16[16,32,128]{2,1,0:...) custom-call(bf16[8,16,16,128]{3,2,1,0:T(8,128)(2,1)} %reshape.173.bl, ...), custom_call_target="tpu_custom_call" | custom-call | flops 1000000000 | bytes 10000000 | tf_op jit(solution)/shard_map/exchange/pallas_call | solution.py:265
  37.6 6.8 %collective-permute-start = (bf16[64,128,128]{2,1,0:T(8,128)(2,1)}, bf16[64,128,128]{2,1,0:T(8,128)(2,1)}, u32[]{:S(2)}, u32[]{:S(2)}) collective-permute-start(bf16[64,128,128]{2,1,0:T(8,128)(2,1)} %bitcast.27), channel_id=1, source_target_pairs={{1,2},{3,4},{5,6},{7,8},{9,10},{11,12},{13,14},{15,16},{17,18},{19... | collective-permute-start | bytes 6291464 | tf_op jit(solution)/shard_map/ppermute | solution.py:592
  44.4 0.0 copy-done.4
  44.4 0.1 convert_reduce_fusion
  44.6 0.1 select_reduce_fusion
  44.7 0.7 copy.30
  45.4 0.7 copy.32
  46.1 1.0 slice_reduce_fusion
  47.1 0.1 eq.117
  47.2 1.0 reshape.179
  48.2 0.2 copy.38
  48.3 0.1 reshape.180
  48.5 1.3 %reshape.176 = bf16[256,1024]{1,0:T(8,128)(2,1)S(1)} reshape(bf16[16,8,16,128]{3,2,1,0:T(8,128)(2,1)} %get-tuple-element.23) | data formatting | bytes 1048576 | tf_op jit(solution)/shard_map/reshape | solution.py:596
  49.7 0.2 copy.33
  50.0 0.3 convolution_bitcast_fusion
  50.3 0.6 copy.34
  50.9 0.0 copy-start.3
  50.9 0.0 copy-start.2
  50.9 1.0 reshape.177
  51.9 0.0 copy-done.3
  51.9 0.0 copy-done.2
  51.9 0.7 pad_add_fusion.near
  52.6 0.6 subtract_convert_fusion.1
  53.2 23.5 %close.1.partial = f32[64,128,128]{2,1,0:T(8,128)} custom-call(s32[64,29]{1,0:T(8,128)} %pad_add_fusion.near, bf16[200,32,128]{2,1,0:T(8,128)(2,1)} %get-tuple-element.18.source, bf16[64,32,128]{2,1,0:T(8,128)(2,1)} %get-tuple-element.19.target, bf16[64,128,128]{2,1,0:T(8,128)(2,1)} %bitcast.28, bf16[64,128,128]{2,1,0:T(8,128)(2,1)} %get-tuple-element.20.partner), custom_call_target="tpu_custom_call" | custom-call | flops 5000000000 | bytes 10000000 | tf_op jit(solution)/shard_map/close/pallas_call | solution.py:489
  76.8 0.9 subtract_convert_fusion
  77.6 0.0 collective-permute-done.other
  77.6 27.7 %near.1 = bf16[8192,128]{1,0:T(8,128)(2,1)} custom-call(s32[64,29]{1,0:T(8,128)} %pad_add_fusion.near, bf16[200,32,128]{2,1,0:T(8,128)(2,1)} %get-tuple-element.18.source, bf16[64,32,128]{2,1,0:T(8,128)(2,1)} %get-tuple-element.19.target, bf16[64,128,128]{2,1,0:T(8,128)(2,1)} %bitcast.29, bf16[64,128,128]{2,1,0:T(8,128)(2,1)} %get-tuple-element.20.partner, ...), custom_call_target="tpu_custom_call" | custom-call | flops 5000000000 | bytes 10000000 | tf_op jit(solution)/shard_map/near/pallas_call | solution.py:522
  (6 shorter events, 0.1 us)
Async XLA Ops:
  0.0 5.6 %copy-start = (bf16[189,1024]{1,0:T(8,128)(2,1)S(1)}, bf16[189,1024]{1,0:T(8,128)(2,1)}, u32[]{:S(2)}) copy-start(bf16[189,1024]{1,0:T(8,128)(2,1)} %param.20) | copy-start | bytes 1161220
  0.0 7.1 %copy-start.1 = (bf16[64,4096]{1,0:T(8,128)(2,1)S(1)}, bf16[64,4096]{1,0:T(8,128)(2,1)}, u32[]{:S(2)}) copy-start(bf16[64,4096]{1,0:T(8,128)(2,1)} %param.16) | copy-start | bytes 1572868
  8.0 36.4 %copy-start.4 = (s32[64,27]{0,1:T(8,128)S(1)}, s32[64,27]{0,1:T(8,128)}, u32[]{:S(2)}) copy-start(s32[64,27]{0,1:T(8,128)} %param.15) | copy-start | bytes 20740
  37.6 40.1 %collective-permute-start = (bf16[64,128,128]{2,1,0:T(8,128)(2,1)}, bf16[64,128,128]{2,1,0:T(8,128)(2,1)}, u32[]{:S(2)}, u32[]{:S(2)}) collective-permute-start(bf16[64,128,128]{2,1,0:T(8,128)(2,1)} %bitcast.27), channel_id=1, source_target_pairs={{1,2},{3,4},{5,6},{7,8},{9,10},{11,12},{13,14},{15,16},{17,18},{19... | collective-permute-start | bytes 6291464 | tf_op jit(solution)/shard_map/ppermute | solution.py:592
  50.9 1.0 copy-start.3
  50.9 1.0 copy-start.2

commit v3 on v2

--- a/solution.py
+++ b/solution.py
@@ -59,7 +59,7 @@
         rows += [*split3(norm + scale * scale * DELTA_SQ), one, one, one]
     else:
         rows += [one, one, one, *split3(norm)]
-    return rows + [jnp.zeros_like(norm)] * (K - len(rows))
+    return rows
 
 
 def exchange_kernel(
@@ -115,6 +115,8 @@
         for l in range(LEAVES):
             points[i, l : l + 1, :] = coords[i : i + 1, l * M : (l + 1) * M]
 
+    lines[...] = jnp.zeros_like(lines)
+
     fetch.wait()
 
     def one_mid(m, c):
@@ -126,7 +128,7 @@
         mids[pl.ds(pl.multiple_of(m * K, K), K), :] = rows.astype(bf16)
         return c
 
-    lax.fori_loop(0, GROUP, one_mid, 0)
+    lax.fori_loop(0, GROUP, one_mid, 0, unroll=2)
     base = dot_t(transfers[LEAVES * K : LEAVES * K + GROUP * K, :], mids[...]).astype(bf16)
     coeffs[0] = base
     coeffs[1] = dot_t(transfers[LEAVES * K + GROUP * K :, :], base).astype(bf16)
@@ -185,7 +187,7 @@
         return lines[pl.ds(pl.multiple_of(l * K, K), K), :]
 
     def put_target(l, c):
-        target[l] = line(l).astype(bf16)
+        target[l] = line(l).T.astype(bf16)
         return c
 
     def put_source(block):
@@ -271,7 +273,7 @@
             shape((16, K, RHS), bf16),
             shape((16, K * K), f32),
             shape((POOL + 8, K, M), bf16),
-            shape((LEAVES, K, M), bf16),
+            shape((LEAVES, M, K), bf16),
             shape((LEAVES, M, RHS), bf16),
         ),
         in_specs=[
@@ -336,29 +338,17 @@
         leaf = step * GROUP + b
         return [(near[leaf, 2 * j], near[leaf, 2 * j + 1], j) for j in range(HALF // 2)]
 
-    def fill(b):
-        mine = target[b].T
+    @pl.when(step == 0)
+    def _():
+        for copy in load_pool((here, partner), pool, sems, 2 * LEAVES):
+            copy.wait()
+
+    for b in range(GROUP):
+        mine = target[b]
         for one, two, j in entries(b):
             kernel_rows(b, mine, one, two, j, source, kern)
-
-    def group(filled):
-        for b in range(GROUP):
-            if not filled:
-                fill(b)
-            for one, two, j in entries(b):
-                charge_rows(b, one, two, j, pool, gathered, 2 * LEAVES)
-            out[b] = dot(kern[b], gathered[b])
-
-    @pl.when(step == 0)
-    def _():
-        copies = load_pool((here, partner), pool, sems, 2 * LEAVES)
-        for b in range(GROUP):
-            fill(b)
-        for copy in copies:
-            copy.wait()
-        group(True)
-
-    pl.when(step > 0)(lambda: group(False))
+            charge_rows(b, one, two, j, pool, gathered, 2 * LEAVES)
+        out[b] = dot(kern[b], gathered[b])
 
 
 def near_kernel(
@@ -394,16 +384,9 @@
             for j in range(HALF // 2)
         ]
 
-    def fill(b):
-        mine = target[b].T
-        for one, two, j in entries(b):
-            kernel_rows(b, mine, one, two, j, source, kern)
-
     @pl.when(step == 0)
     def _():
         copies = load_pool((here, partner, other), pool, sems, POOL)
-        for b in range(GROUP):
-            fill(b)
         extra[...] = jnp.zeros_like(extra)
         top_field = (dot(t_high[...], top_all[...]) + dot(t_low[...], top_all[...])).astype(bf16)
         coupled = dot(a_high[...], every[...]) + dot(a_low[...], every[...])
@@ -422,7 +405,7 @@
 
             def one_entry(e, total):
                 g = near[leaf, e]
-                squares = dot_t(target[b], source[g])
+                squares = dot(target[b], source[g])
                 return total + dot(lax.rsqrt(squares.astype(bf16)), pool[g])
 
             extra[b] = lax.fori_loop(
@@ -432,22 +415,18 @@
 
         lax.fori_loop(0, GROUP, one_leaf, 0)
 
-    def group(filled):
-        down = transfers[pl.ds(pl.multiple_of((LEAVES + step) * K, K), K), :]
-        mid = dot(down, base[...]).astype(bf16)
-        down = transfers[pl.ds(pl.multiple_of(step * GROUP * K, GROUP * K), GROUP * K), :]
-        fields = dot(down, mid).astype(bf16)
-        for b in range(GROUP):
-            if not filled:
-                fill(b)
-            for one, two, j in entries(b):
-                charge_rows(b, one, two, j, pool, gathered, POOL)
-            far = dot_t(basis[b], fields[b * K : (b + 1) * K])
-            total = dot(kern[b], gathered[b]) + far + (partial[b] + extra[b])
-            out[pl.ds(b * M, M), :] = total.astype(bf16)
-
-    pl.when(step == 0)(lambda: group(True))
-    pl.when(step > 0)(lambda: group(False))
+    down = transfers[pl.ds(pl.multiple_of((LEAVES + step) * K, K), K), :]
+    mid = dot(down, base[...]).astype(bf16)
+    down = transfers[pl.ds(pl.multiple_of(step * GROUP * K, GROUP * K), GROUP * K), :]
+    fields = dot(down, mid).astype(bf16)
+    for b in range(GROUP):
+        mine = target[b]
+        for one, two, j in entries(b):
+            kernel_rows(b, mine, one, two, j, source, kern)
+            charge_rows(b, one, two, j, pool, gathered, POOL)
+        far = dot_t(basis[b], fields[b * K : (b + 1) * K])
+        total = dot(kern[b], gathered[b]) + far + (partial[b] + extra[b])
+        out[pl.ds(b * M, M), :] = total.astype(bf16)
 
     @pl.when(late > 0)
     def _():
@@ -479,7 +458,7 @@
         grid=(LEAVES // GROUP,),
         in_specs=[
             vmem(*source.shape),
-            pl.BlockSpec((GROUP, K, M), lambda i, _: (i, 0, 0)),
+            pl.BlockSpec((GROUP, M, K), lambda i, _: (i, 0, 0)),
             anywhere,
             anywhere,
         ],
@@ -502,7 +481,7 @@
         grid=(LEAVES // GROUP,),
         in_specs=[
             vmem(*source.shape),
-            pl.BlockSpec((GROUP, K, M), lambda i, _: (i, 0, 0)),
+            pl.BlockSpec((GROUP, M, K), lambda i, _: (i, 0, 0)),
             anywhere,
             anywhere,
             anywhere,

time: 108 us -> 106 us (0.981)
  Pallas kernels: 80.3 us -> 78.7 us
where the time goes in v3:
time: 106 us; the launch traced here: 105 us
  Pallas kernels  78.7 us (74%)
  local copies, waits for them, and re-layouts  10.9 us (10%)
  starting transfers between devices  7.4 us (7%)
  other arithmetic  6.44 us (6%)
    pallas_call x1, Pallas kernels, exchange_call(): pl.pallas_call(functools.partial(exchange_kernel, math.sqrt(NNEAR * M)),...  28.8 us
    pallas_call x1, Pallas kernels, near_call(): pl.pallas_call(near_kernel, grid_spec=grid_spec, out_shape=jax.ShapeDtype...  27 us
    pallas_call x1, Pallas kernels, close_call(): pl.pallas_call(close_kernel, grid_spec=grid_spec, out_shape=jax.ShapeDtyp...  22.9 us
    ppermute x1, starting transfers between devices, per_device(): other = lax.ppermute(sent, AXIS, outward)  7.4 us
  transfers between devices with their start and end apart: 1, of which 0 were waited for; matrix products, arithmetic and copies ran while one was open for 9% of the time, Pallas kernels for 22%

profile of v3, /device:TPU:32, one launch (start us, length us, event | category | flops | bytes accessed | tf_op | source)
XLA Modules:
  0.0 104.5 jit_solution(16774920877287755063)
XLA Ops:
  0.0 0.0 copy-start
  0.0 0.0 copy-start.1
  0.0 1.0 convert_reduce_fusion.1
  1.0 0.7 fusion.14
  1.7 0.1 multiply_reduce_fusion
  1.8 0.7 multiply_add_fusion.1
  2.5 0.1 tile.10
  2.6 0.1 sub.65
  2.7 0.7 pad.4.blk_src
  3.4 1.0 pad_maximum_fusion
  4.4 1.3 %reshape.175.transfers = bf16[2336,32]{1,0:T(8,128)(2,1)} reshape(bf16[73,1024]{1,0:T(8,128)(2,1)S(1)} %pad_maximum_fusion) | data formatting | bytes 299008 | tf_op jit(solution)/shard_map/reshape | solution.py:565
  5.6 0.0 copy-done
  5.6 0.4 convolution_convert_fusion
  6.1 1.0 reshape.173.blk
  7.1 0.0 copy-done.1
  7.1 0.9 copy.36
  8.0 0.0 copy-start.4
  8.0 0.6 compare_select_fusion.2.top_idx
  8.6 28.8 %exchange.1 = (bf16[16,8,16,128]{3,2,1,0:T(8,128)(2,1)}, s32[16,8,1,128]{3,2,1,0:T(1,128)}, bf16[2,16,4,32,128]{4,3,2,1,0:T(8,128)(2,1)}, bf16[16,32,128]{2,1,0:...) custom-call(bf16[8,16,16,128]{3,2,1,0:T(8,128)(2,1)} %reshape.173.bl, ...), custom_call_target="tpu_custom_call" | custom-call | flops 1000000000 | bytes 10000000 | tf_op jit(solution)/shard_map/exchange/pallas_call | solution.py:267
  37.4 7.4 %collective-permute-start = (bf16[64,128,128]{2,1,0:T(8,128)(2,1)}, bf16[64,128,128]{2,1,0:T(8,128)(2,1)}, u32[]{:S(2)}, u32[]{:S(2)}) collective-permute-start(bf16[64,128,128]{2,1,0:T(8,128)(2,1)} %bitcast.24), channel_id=1, source_target_pairs={{1,2},{3,4},{5,6},{7,8},{9,10},{11,12},{13,14},{15,16},{17,18},{19... | collective-permute-start | bytes 6291464 | tf_op jit(solution)/shard_map/ppermute | solution.py:571
  44.8 0.0 copy-done.4
  44.9 0.1 convert_reduce_fusion
  45.0 0.1 select_reduce_fusion
  45.1 0.7 copy.30
  45.8 0.7 copy.32
  46.5 1.0 slice_reduce_fusion
  47.5 0.1 eq.117
  47.7 1.0 reshape.179
  48.6 0.2 copy.38
  48.8 0.1 reshape.180
  48.9 1.3 %reshape.176 = bf16[256,1024]{1,0:T(8,128)(2,1)S(1)} reshape(bf16[16,8,16,128]{3,2,1,0:T(8,128)(2,1)} %get-tuple-element.23) | data formatting | bytes 1048576 | tf_op jit(solution)/shard_map/reshape | solution.py:575
  50.2 0.2 copy.33
  50.4 0.3 convolution_bitcast_fusion
  50.7 0.6 copy.34
  51.3 0.0 copy-start.3
  51.3 0.0 copy-start.2
  51.4 1.0 reshape.177
  52.3 0.0 copy-done.3
  52.3 0.0 copy-done.2
  52.3 0.7 pad_add_fusion.near
  53.0 0.6 subtract_convert_fusion.1
  53.7 22.9 %close.1.partial = f32[64,128,128]{2,1,0:T(8,128)} custom-call(s32[64,29]{1,0:T(8,128)} %pad_add_fusion.near, bf16[200,32,128]{2,1,0:T(8,128)(2,1)} %get-tuple-element.18.source, bf16[64,128,32]{2,1,0:T(8,128)(2,1)} %get-tuple-element.19.target, bf16[64,128,128]{2,1,0:T(8,128)(2,1)} %bitcast.25, bf16[64,128,128]{2,1,0:T(8,128)(2,1)} %get-tuple-element.20.partner), custom_call_target="tpu_custom_call" | custom-call | flops 5000000000 | bytes 10000000 | tf_op jit(solution)/shard_map/close/pallas_call | solution.py:468
  76.5 0.8 subtract_convert_fusion
  77.4 0.0 collective-permute-done.other
  77.4 27.0 %near.1 = bf16[8192,128]{1,0:T(8,128)(2,1)} custom-call(s32[64,29]{1,0:T(8,128)} %pad_add_fusion.near, bf16[200,32,128]{2,1,0:T(8,128)(2,1)} %get-tuple-element.18.source, bf16[64,128,32]{2,1,0:T(8,128)(2,1)} %get-tuple-element.19.target, bf16[64,128,128]{2,1,0:T(8,128)(2,1)} %bitcast.26, bf16[64,128,128]{2,1,0:T(8,128)(2,1)} %get-tuple-element.20.partner, ...), custom_call_target="tpu_custom_call" | custom-call | flops 5000000000 | bytes 10000000 | tf_op jit(solution)/shard_map/near/pallas_call | solution.py:501
  (6 shorter events, 0.1 us)
Async XLA Ops:
  0.0 5.6 %copy-start = (bf16[189,1024]{1,0:T(8,128)(2,1)S(1)}, bf16[189,1024]{1,0:T(8,128)(2,1)}, u32[]{:S(2)}) copy-start(bf16[189,1024]{1,0:T(8,128)(2,1)} %param.20) | copy-start | bytes 1161220
  0.0 7.1 %copy-start.1 = (bf16[64,4096]{1,0:T(8,128)(2,1)S(1)}, bf16[64,4096]{1,0:T(8,128)(2,1)}, u32[]{:S(2)}) copy-start(bf16[64,4096]{1,0:T(8,128)(2,1)} %param.16) | copy-start | bytes 1572868
  8.0 36.9 %copy-start.4 = (s32[64,27]{0,1:T(8,128)S(1)}, s32[64,27]{0,1:T(8,128)}, u32[]{:S(2)}) copy-start(s32[64,27]{0,1:T(8,128)} %param.15) | copy-start | bytes 20740
  37.4 39.9 %collective-permute-start = (bf16[64,128,128]{2,1,0:T(8,128)(2,1)}, bf16[64,128,128]{2,1,0:T(8,128)(2,1)}, u32[]{:S(2)}, u32[]{:S(2)}) collective-permute-start(bf16[64,128,128]{2,1,0:T(8,128)(2,1)} %bitcast.24), channel_id=1, source_target_pairs={{1,2},{3,4},{5,6},{7,8},{9,10},{11,12},{13,14},{15,16},{17,18},{19... | collective-permute-start | bytes 6291464 | tf_op jit(solution)/shard_map/ppermute | solution.py:571
  51.3 1.0 copy-start.3
  51.3 1.0 copy-start.2

commit v4 on v3

--- a/solution.py
+++ b/solution.py
@@ -17,6 +17,7 @@
 NNEAR = 27
 HALF = (NNEAR + 1) // 2
 GROUP = 8
+WIDE = 16
 DELTA_SQ = 0.0025
 AXIS = "leaf"
 MESH = pl.DeviceIdType.MESH
@@ -335,7 +336,7 @@
     step = pl.program_id(0)
 
     def entries(b):
-        leaf = step * GROUP + b
+        leaf = step * WIDE + b
         return [(near[leaf, 2 * j], near[leaf, 2 * j + 1], j) for j in range(HALF // 2)]
 
     @pl.when(step == 0)
@@ -343,7 +344,7 @@
         for copy in load_pool((here, partner), pool, sems, 2 * LEAVES):
             copy.wait()
 
-    for b in range(GROUP):
+    for b in range(WIDE):
         mine = target[b]
         for one, two, j in entries(b):
             kernel_rows(b, mine, one, two, j, source, kern)
@@ -433,11 +434,11 @@
         extra[...] = jnp.zeros_like(extra)
 
 
-def near_scratch(leaves):
+def near_scratch(leaves, group):
     return [
         pltpu.VMEM((leaves, M, RHS), bf16),
-        pltpu.VMEM((GROUP, M, M * HALF), bf16),
-        pltpu.VMEM((GROUP, M * HALF, RHS), bf16),
+        pltpu.VMEM((group, M, M * HALF), bf16),
+        pltpu.VMEM((group, M * HALF, RHS), bf16),
     ]
 
 
@@ -455,15 +456,15 @@
     anywhere = pl.BlockSpec(memory_space=pl.ANY)
     grid_spec = pltpu.PrefetchScalarGridSpec(
         num_scalar_prefetch=1,
-        grid=(LEAVES // GROUP,),
+        grid=(LEAVES // WIDE,),
         in_specs=[
             vmem(*source.shape),
-            pl.BlockSpec((GROUP, M, K), lambda i, _: (i, 0, 0)),
+            pl.BlockSpec((WIDE, M, K), lambda i, _: (i, 0, 0)),
             anywhere,
             anywhere,
         ],
-        out_specs=pl.BlockSpec((GROUP, M, RHS), lambda i, _: (i, 0, 0)),
-        scratch_shapes=[*near_scratch(2 * LEAVES + 1), pltpu.SemaphoreType.DMA((2,))],
+        out_specs=pl.BlockSpec((WIDE, M, RHS), lambda i, _: (i, 0, 0)),
+        scratch_shapes=[*near_scratch(2 * LEAVES + 1, WIDE), pltpu.SemaphoreType.DMA((2,))],
     )
     return pl.pallas_call(
         close_kernel,
@@ -492,7 +493,7 @@
         ],
         out_specs=pl.BlockSpec((GROUP * M, RHS), lambda i, _: (i, 0)),
         scratch_shapes=[
-            *near_scratch(POOL + 1),
+            *near_scratch(POOL + 1, GROUP),
             pltpu.VMEM((K, RHS), bf16),
             pltpu.VMEM((GROUP, M, RHS), f32),
             pltpu.SemaphoreType.DMA((3,)),

time: 106 us -> 106 us (level)
  transfers between devices with their start and end apart: 1 -> 1, of which waited for: 0 -> 0; matrix products, arithmetic and copies ran while one was open for 9% -> 9% of each run, Pallas kernels for 22% -> 21%
where the time goes in v4:
time: 106 us; the launch traced here: 105 us
  Pallas kernels  78.9 us (74%)
  local copies, waits for them, and re-layouts  10.9 us (10%)
  starting transfers between devices  7.4 us (7%)
  other arithmetic  6.44 us (6%)
    pallas_call x1, Pallas kernels, exchange_call(): pl.pallas_call(functools.partial(exchange_kernel, math.sqrt(NNEAR * M)),...  28.8 us
    pallas_call x1, Pallas kernels, near_call(): pl.pallas_call(near_kernel, grid_spec=grid_spec, out_shape=jax.ShapeDtype...  27.8 us
    pallas_call x1, Pallas kernels, close_call(): pl.pallas_call(close_kernel, grid_spec=grid_spec, out_shape=jax.ShapeDtyp...  22.4 us
    ppermute x1, starting transfers between devices, per_device(): other = lax.ppermute(sent, AXIS, outward)  7.4 us
  transfers between devices with their start and end apart: 1, of which 0 were waited for; matrix products, arithmetic and copies ran while one was open for 9% of the time, Pallas kernels for 21%

profile of v4, /device:TPU:32, one launch (start us, length us, event | category | flops | bytes accessed | tf_op | source)
XLA Modules:
  0.0 104.8 jit_solution(4019192515276498012)
XLA Ops:
  0.0 0.0 copy-start
  0.0 0.0 copy-start.1
  0.0 1.0 convert_reduce_fusion.1
  1.0 0.7 fusion.14
  1.7 0.1 multiply_reduce_fusion
  1.8 0.7 multiply_add_fusion.1
  2.5 0.1 tile.10
  2.6 0.1 sub.65
  2.7 0.7 pad.4.blk_src
  3.4 1.0 pad_maximum_fusion
  4.4 1.3 %reshape.175.transfers = bf16[2336,32]{1,0:T(8,128)(2,1)} reshape(bf16[73,1024]{1,0:T(8,128)(2,1)S(1)} %pad_maximum_fusion) | data formatting | bytes 299008 | tf_op jit(solution)/shard_map/reshape | solution.py:566
  5.6 0.0 copy-done
  5.6 0.4 convolution_convert_fusion
  6.1 1.0 reshape.173.blk
  7.1 0.0 copy-done.1
  7.1 0.9 copy.36
  8.0 0.0 copy-start.4
  8.0 0.6 compare_select_fusion.2.top_idx
  8.6 28.8 %exchange.1 = (bf16[16,8,16,128]{3,2,1,0:T(8,128)(2,1)}, s32[16,8,1,128]{3,2,1,0:T(1,128)}, bf16[2,16,4,32,128]{4,3,2,1,0:T(8,128)(2,1)}, bf16[16,32,128]{2,1,0:...) custom-call(bf16[8,16,16,128]{3,2,1,0:T(8,128)(2,1)} %reshape.173.bl, ...), custom_call_target="tpu_custom_call" | custom-call | flops 1000000000 | bytes 10000000 | tf_op jit(solution)/shard_map/exchange/pallas_call | solution.py:268
  37.4 7.4 %collective-permute-start = (bf16[64,128,128]{2,1,0:T(8,128)(2,1)}, bf16[64,128,128]{2,1,0:T(8,128)(2,1)}, u32[]{:S(2)}, u32[]{:S(2)}) collective-permute-start(bf16[64,128,128]{2,1,0:T(8,128)(2,1)} %bitcast.24), channel_id=1, source_target_pairs={{1,2},{3,4},{5,6},{7,8},{9,10},{11,12},{13,14},{15,16},{17,18},{19... | collective-permute-start | bytes 6291464 | tf_op jit(solution)/shard_map/ppermute | solution.py:572
  44.8 0.0 copy-done.4
  44.9 0.1 convert_reduce_fusion
  45.0 0.1 select_reduce_fusion
  45.1 0.7 copy.30
  45.8 0.7 copy.32
  46.5 1.0 slice_reduce_fusion
  47.5 0.1 eq.117
  47.7 1.0 reshape.179
  48.6 0.2 copy.38
  48.8 0.1 reshape.180
  48.9 1.3 %reshape.176 = bf16[256,1024]{1,0:T(8,128)(2,1)S(1)} reshape(bf16[16,8,16,128]{3,2,1,0:T(8,128)(2,1)} %get-tuple-element.23) | data formatting | bytes 1048576 | tf_op jit(solution)/shard_map/reshape | solution.py:576
  50.2 0.2 copy.33
  50.4 0.3 convolution_bitcast_fusion
  50.7 0.6 copy.34
  51.3 0.0 copy-start.3
  51.3 0.0 copy-start.2
  51.4 1.0 reshape.177
  52.3 0.0 copy-done.3
  52.3 0.0 copy-done.2
  52.3 0.7 pad_add_fusion.near
  53.0 0.6 subtract_convert_fusion.1
  53.7 22.4 %close.1.partial = f32[64,128,128]{2,1,0:T(8,128)} custom-call(s32[64,29]{1,0:T(8,128)} %pad_add_fusion.near, bf16[200,32,128]{2,1,0:T(8,128)(2,1)} %get-tuple-element.18.source, bf16[64,128,32]{2,1,0:T(8,128)(2,1)} %get-tuple-element.19.target, bf16[64,128,128]{2,1,0:T(8,128)(2,1)} %bitcast.25, bf16[64,128,128]{2,1,0:T(8,128)(2,1)} %get-tuple-element.20.partner), custom_call_target="tpu_custom_call" | custom-call | flops 5000000000 | bytes 10000000 | tf_op jit(solution)/shard_map/close/pallas_call | solution.py:469
  76.0 0.8 subtract_convert_fusion
  76.9 0.0 collective-permute-done.other
  76.9 27.8 %near.1 = bf16[8192,128]{1,0:T(8,128)(2,1)} custom-call(s32[64,29]{1,0:T(8,128)} %pad_add_fusion.near, bf16[200,32,128]{2,1,0:T(8,128)(2,1)} %get-tuple-element.18.source, bf16[64,128,32]{2,1,0:T(8,128)(2,1)} %get-tuple-element.19.target, bf16[64,128,128]{2,1,0:T(8,128)(2,1)} %bitcast.26, bf16[64,128,128]{2,1,0:T(8,128)(2,1)} %get-tuple-element.20.partner, ...), custom_call_target="tpu_custom_call" | custom-call | flops 5000000000 | bytes 10000000 | tf_op jit(solution)/shard_map/near/pallas_call | solution.py:502
  (6 shorter events, 0.1 us)
Async XLA Ops:
  0.0 5.6 %copy-start = (bf16[189,1024]{1,0:T(8,128)(2,1)S(1)}, bf16[189,1024]{1,0:T(8,128)(2,1)}, u32[]{:S(2)}) copy-start(bf16[189,1024]{1,0:T(8,128)(2,1)} %param.20) | copy-start | bytes 1161220
  0.0 7.1 %copy-start.1 = (bf16[64,4096]{1,0:T(8,128)(2,1)S(1)}, bf16[64,4096]{1,0:T(8,128)(2,1)}, u32[]{:S(2)}) copy-start(bf16[64,4096]{1,0:T(8,128)(2,1)} %param.16) | copy-start | bytes 1572868
  8.0 36.9 %copy-start.4 = (s32[64,27]{0,1:T(8,128)S(1)}, s32[64,27]{0,1:T(8,128)}, u32[]{:S(2)}) copy-start(s32[64,27]{0,1:T(8,128)} %param.15) | copy-start | bytes 20740
  37.4 39.4 %collective-permute-start = (bf16[64,128,128]{2,1,0:T(8,128)(2,1)}, bf16[64,128,128]{2,1,0:T(8,128)(2,1)}, u32[]{:S(2)}, u32[]{:S(2)}) collective-permute-start(bf16[64,128,128]{2,1,0:T(8,128)(2,1)} %bitcast.24), channel_id=1, source_target_pairs={{1,2},{3,4},{5,6},{7,8},{9,10},{11,12},{13,14},{15,16},{17,18},{19... | collective-permute-start | bytes 6291464 | tf_op jit(solution)/shard_map/ppermute | solution.py:572
  51.3 1.0 copy-start.3
  51.3 1.0 copy-start.2
